TPU v7x, 32 devices: a whole 2x2x4 slice. The times are simulated.
32 devices in a mesh: band: 8 (over y, x, core), ga: 4 (over z).
Axes of the slice: x: 2, y: 2, z: 4, core: 2. Of those that a mesh axis runs over, the one named last changes fastest.
Arguments:
- wave_coef: bfloat16 [4096, 16384], P('band', 'ga'), may hold values from -0.046875 to 0.046875
- projector: bfloat16 [32, 27, 16384], P('band', None, 'ga'), may hold values from -6 to 6
- occupation: float32 [4096], P('band'), may hold values from 0.25 to 4
- species: int32 [32], replicated, may hold values from 0 to 3
- layer_in: float32 [4, 729, 100], replicated, may hold values from -1.25 to 1.25
- bias_in: float32 [4, 100], replicated, may hold values from -3 to 3
- layer_out: float32 [4, 100], replicated, may hold values from -0.625 to 0.625
Outputs:
- corrected: bfloat16 [4096, 16384], P('band', 'ga')
All inputs are finite; a program needn't handle non-finite values.
Results may differ from a plain program's by a relative error of at most 0.0049.
Values may be sent and summed in bfloat16 or wider, within the bound.
A program may use at most 128 MiB of HBM per device.

v0:
```python
import jax
import jax.numpy as jnp
from jax import lax
from jax.sharding import PartitionSpec as P


def descriptor_step(density, kinds, layer_in, bias_in, layer_out, orbitals):
    atoms_here = density.shape[0]
    nspecies = layer_in.shape[0]
    onehot = (kinds[:, None] == jnp.arange(nspecies, dtype=jnp.int32)[None, :]).astype(jnp.float32)
    weight_atom = jnp.einsum("as,sfh->afh", onehot, layer_in, precision=lax.Precision.HIGHEST)
    bias_atom = jnp.dot(onehot, bias_in, precision=lax.Precision.HIGHEST)
    out_atom = jnp.dot(onehot, layer_out, precision=lax.Precision.HIGHEST)
    preact = (
        jnp.einsum(
            "af,afh->ah",
            density.reshape(atoms_here, orbitals * orbitals),
            weight_atom,
            precision=lax.Precision.HIGHEST,
        )
        + bias_atom
    )
    activation = jnp.tanh(preact)
    slopes = out_atom * (1.0 - activation * activation)
    gradient = jnp.einsum(
        "afh,ah->af", weight_atom, slopes, precision=lax.Precision.HIGHEST
    ).reshape(atoms_here, orbitals, orbitals)
    return gradient + jnp.swapaxes(gradient, 1, 2)


def project(wave_coef, segment):
    return jnp.einsum("ng,akg->nak", wave_coef, segment, preferred_element_type=jnp.float32)


def body(wave_coef, projector, occupation, species, layer_in, bias_in, layer_out):
    orbitals = projector.shape[1]
    atoms_all = projector.shape[0] * lax.axis_size("band")
    bands_all = wave_coef.shape[0] * lax.axis_size("band")
    whole_proj = lax.all_gather(projector, "band", axis=0, tiled=True)
    partial_value = project(wave_coef, whole_proj)
    coefficient = lax.psum_scatter(partial_value, "ga", scatter_dimension=1, tiled=True)
    owned = coefficient.shape[1]
    first_atom = lax.axis_index("ga") * owned
    local_density = jnp.einsum(
        "n,nak,nal->akl", occupation, coefficient, coefficient, precision=lax.Precision.HIGHEST
    )
    density = lax.psum(local_density, "band") / bands_all
    kinds = lax.dynamic_slice_in_dim(species, first_atom, owned, 0)
    symmetric = descriptor_step(density, kinds, layer_in, bias_in, layer_out, orbitals)
    factor = 1.0 / jnp.sqrt(jnp.float32(atoms_all * orbitals))
    applied = (
        jnp.einsum("akl,nal->nak", symmetric, coefficient, precision=lax.Precision.HIGHEST) * factor
    ).astype(jnp.bfloat16)
    applied_all = lax.all_gather(applied, "ga", axis=1, tiled=True)
    corrected = jnp.einsum(
        "nak,akg->ng", applied_all, whole_proj, preferred_element_type=jnp.float32
    )
    return corrected.astype(jnp.bfloat16)


def solution(mesh):
    in_specs = (P("band", "ga"), P("band", None, "ga"), P("band"), P(), P(), P(), P())
    out_specs = P("band", "ga")
    return jax.shard_map(body, mesh=mesh, in_specs=in_specs, out_specs=out_specs, check_vma=False)
```

profile of v0, /device:TPU:0, one launch (start us, length us, event | category | flops | bytes accessed | tf_op | source)
XLA Modules:
  0.0 195.1 jit_solution(14099353177213879075)
XLA Ops:
  6.5 0.0 copy-start
  6.5 0.0 all-gather.2.cloned.1.call-start
  6.5 2.7 %copy.22 = bf16[4,27,4096]{2,1,0:T(8,128)(2,1)} copy(bf16[4,27,4096]{2,0,1:T(4,128)(2,1)} %param.8) | data formatting | bytes 1769472 | tf_op args[1]
  9.3 0.0 all-gather.2.cloned.1.call-update
  9.3 0.0 copy-start.5
  9.3 0.0 copy-start.3
  9.3 0.0 reduce-scatter.2.cloned.1.call-start
  9.4 57.1 %all-gather.2.cloned.1.call-done = bf16[32,27,4096]{2,1,0:T(8,128)(2,1)} async-done(((bf16[4,27,4096]{2,1,0:T(8,128)(2,1)}), bf16[32,27,4096]{2,1,0:T(8,128)(2,1)}) %all-gather.2.cloned.1.call-update) | async-done | bytes 7077904 | tf_op jit(solution)/shard_map/all_gather | solution.py:39
  66.4 10.6 %fusion.1 = f32[512,32,27]{0,1,2:T(8,128)} fusion(bf16[32,27,4096]{2,1,0:T(8,128)(2,1)} %all-gather.2.cloned.1.call-done, bf16[512,4096]{1,0:T(8,128)(2,1)} %param.7), kind=kOutput, calls=%fused_computation.2 | convolution fusion | flops 3623878656 | bytes 13041664 | tf_op jit(solution)/shard_map/ng,akg->nak/dot_general | solution.py:32
  77.1 0.0 copy-start.2
  77.1 0.0 reduce-scatter.2.cloned.1.call-update
  77.1 0.0 copy-done.5
  77.1 0.1 dynamic_slice.3
  77.2 0.0 copy-done.3
  77.2 0.2 fusion.18
  77.4 0.0 copy-done
  77.4 0.0 copy-start.4
  77.4 3.0 %fusion.20 = f32[8,729,100]{1,0,2:T(8,128)} fusion(f32[4,729,100]{1,0,2:T(4,128)S(1)} %copy-done, s32[8]{0:T(128)S(1)} %dynamic_slice.3), kind=kOutput, calls=%fused_computation.28 | convolution fusion | flops 27993632 | bytes 3499232 | tf_op jit(solution)/shard_map/as,sfh->afh/dot_general | solution.py:11
  80.3 35.4 %reduce-scatter.2.cloned.1.call-done = f32[512,8,27]{0,1,2:T(8,128)} async-done(((f32[512,32,27]{0,1,2:T(8,128)}), f32[512,8,27]{0,1,2:T(8,128)}) %reduce-scatter.2.cloned.1.call-update) | async-done | bytes 442384 | tf_op jit(solution)/shard_map/reduce_scatter | solution.py:41
  115.7 0.0 copy-done.2
  115.7 0.0 copy-start.1
  115.7 1.1 broadcast_multiply_fusion
  116.8 2.1 %fusion.14 = f32[8,27,27]{2,1,0:T(8,128)S(1)} fusion(f32[512,8,27]{0,1,2:T(8,128)} %reduce-scatter.2.cloned.1.call-done, f32[512,8,27]{0,1,2:T(8,128)S(1)} %broadcast_multiply_fusion), kind=kOutput, calls=%fused_computation.17 | convolution fusion | flops 35831808 | bytes 908064 | tf_op jit(solution)/shard_map/n,nak,nal->akl/dot_general | solution.py:44
  119.0 25.0 %psum.7 = f32[8,27,27]{2,1,0:T(8,128)S(1)} all-reduce(f32[8,27,27]{2,1,0:T(8,128)S(1)} %fusion.14), channel_id=1, replica_groups=mesh['band'=8,'ga'=4] {'band'}, use_global_device_ids=true, to_apply=%region_1.0 | all-reduce | flops 5832 | bytes 46656 | tf_op jit(solution)/shard_map/psum | solution.py:47
  144.0 0.1 reshape.17
  144.2 4.3 %fusion.6 = f32[8,1,100]{2,1,0:T(1,128)S(1)} fusion(f32[8,729,1]{1,2,0:T(1,128)S(1)} %reshape.17, f32[8,729,100]{1,0,2:T(8,128)} %fusion.20), kind=kOutput, calls=%fused_computation.7 | convolution fusion | flops 6998400 | bytes 2359328 | tf_op jit(solution)/shard_map/af,afh->ah/dot_general | solution.py:15
  148.5 0.0 copy-done.4
  148.5 0.2 fusion.13
  148.7 3.9 %fusion.4 = f32[8,1,729]{2,1,0:T(1,128)S(1)} fusion(f32[8,100,1]{1,2,0:T(1,128)S(1)} %bitcast.28, f32[8,729,100]{1,0,2:T(8,128)} %fusion.20), kind=kOutput, calls=%fused_computation.5 | convolution fusion | flops 6998400 | bytes 2359328 | tf_op jit(solution)/shard_map/afh,ah->af/dot_general | solution.py:25
  152.7 0.1 reshape.8
  152.8 0.1 copy.26
  152.9 0.0 copy-done.1
  152.9 0.9 fusion.9
  153.9 0.1 copy.28
  154.0 18.6 %all_gather.7 = bf16[512,32,27]{0,1,2:T(8,128)(2,1)S(1)} all-gather(bf16[512,8,27]{0,1,2:T(8,128)(2,1)S(1)} %copy.28), channel_id=1, replica_groups=mesh['band'=8,'ga'=4] {'ga'}, dimensions={1}, use_global_device_ids=true | all-gather | bytes 1105920 | tf_op jit(solution)/shard_map/all_gather | solution.py:54
  172.6 15.7 %bitcast_convert_fusion = bf16[512,4096]{1,0:T(8,128)(2,1)} fusion(bf16[512,32,27]{0,1,2:T(8,128)(2,1)S(1)} %all_gather.7, bf16[32,27,4096]{2,1,0:T(8,128)(2,1)} %all-gather.2.cloned.1.call-done), kind=kOutput, calls=%fused_computation | convolution fusion | flops 3625975808 | bytes 12156928 | tf_op jit(solution)/shard_map/nak,akg->ng/dot_general | solution.py:55
  (2 shorter events, 0.0 us)
Async XLA Ops:
  6.5 70.8 %copy-start = (f32[4,729,100]{1,0,2:T(4,128)S(1)}, f32[4,729,100]{1,0,2:T(4,128)}, u32[]{:S(2)}) copy-start(f32[4,729,100]{1,0,2:T(4,128)} %param.11) | copy-start | bytes 3499204
  6.5 59.9 %all-gather.2.cloned.1.call-start = ((), (), s32[]{:S(2)}) async-start(), calls=%async_computation.1 | async-start | bytes 9437184 | tf_op jit(solution)/shard_map/all_gather | solution.py:39
  9.3 67.8 %copy-start.5 = (s32[32]{0:T(128)S(1)}, s32[32]{0:T(128)}, u32[]{:S(2)}) copy-start(s32[32]{0:T(128)} %param.10) | copy-start | bytes 388
  9.3 67.9 %copy-start.3 = (f32[4,100]{1,0:T(4,128)S(1)}, f32[4,100]{1,0:T(4,128)}, u32[]{:S(2)}) copy-start(f32[4,100]{1,0:T(4,128)} %param.13) | copy-start | bytes 4804
  9.3 106.4 %reduce-scatter.2.cloned.1.call-start = ((), (), s32[]{:S(2)}) async-start(), calls=%async_computation.2 | async-start | bytes 2211840 | tf_op jit(solution)/shard_map/reduce_scatter | solution.py:41
  77.1 38.7 %copy-start.2 = (f32[512]{0:T(512)S(1)}, f32[512]{0:T(512)}, u32[]{:S(2)}) copy-start(f32[512]{0:T(512)} %param.9) | copy-start | bytes 6148
  77.4 71.1 %copy-start.4 = (f32[4,100]{1,0:T(4,128)S(1)}, f32[4,100]{1,0:T(4,128)}, u32[]{:S(2)}) copy-start(f32[4,100]{1,0:T(4,128)} %param.12) | copy-start | bytes 4804
  115.7 37.2 %copy-start.1 = (f32[512,8,27]{0,1,2:T(8,128)S(1)}, f32[512,8,27]{0,1,2:T(8,128)}, u32[]{:S(2)}) copy-start(f32[512,8,27]{0,1,2:T(8,128)} %reduce-scatter.2.cloned.1.call-done) | copy-start | bytes 1327108
Sparse Core Ops, SparseCore 0:
  9.4 56.9 all-gather.1
  77.2 38.4 reduce-scatter.1
where the time goes:
time: 195 us
  waiting for transfers between devices  92.5 us (47%)
  blocking collectives  43.6 us (22%)
  matrix products  41 us (21%)
  between operations  13.5 us (7%)
  local copies, waits for them, and re-layouts  3.39 us (2%)
    all_gather x1, waiting for transfers between devices, body(): whole_proj = lax.all_gather(projector, 'band', axis=0, tiled=True)  57.1 us
    reduce_scatter x1, waiting for transfers between devices, body(): lax.psum_scatter(partial_value, 'ga', scatter_dimension=1, tiled=True)  35.4 us
    psum x1, blocking collectives, body(): density = lax.psum(local_density, 'band') / bands_all  25 us
    all_gather x1, blocking collectives, body(): applied_all = lax.all_gather(applied, 'ga', axis=1, tiled=True)  18.6 us
    dot_general x1, matrix products, body(): jnp.einsum('nak,akg->ng', applied_all, whole_proj, preferred_element_type...  15.7 us
    dot_general x1, matrix products, project(): jnp.einsum('ng,akg->nak', wave_coef, segment, preferred_element_type=jnp....  10.6 us
    dot_general x1, matrix products, descriptor_step(): jnp.einsum('af,afh->ah', density.reshape(atoms_here, orbitals * orbitals)...  4.34 us
    dot_general x1, matrix products, descriptor_step(): jnp.einsum('afh,ah->af', weight_atom, slopes, precision=lax.Precision.HIG...  3.93 us
  transfers between devices with their start and end apart: 2, of which 2 were waited for; matrix products, arithmetic and copies ran while one was open for 2% of the time, Pallas kernels for 0%

commit v1 on v0

v1 whole, which is shorter than its diff:
```python
import functools

import jax
import jax.numpy as jnp
from jax import lax
from jax.experimental import pallas as pl
from jax.experimental.pallas import tpu as pltpu
from jax.sharding import PartitionSpec as P

MESH = pl.DeviceIdType.MESH
F32 = jnp.float32
BF16 = jnp.bfloat16
PIECES = 4
LPAD = 32


def split(value):
    high = value.astype(BF16)
    return high, (value - high.astype(F32)).astype(BF16)


def dot(a, b, contract):
    return lax.dot_general(a, b, ((contract[:1], contract[1:]), ((), ())), preferred_element_type=F32)


def kernel(dims, wave_hbm, proj_hbm, occ_ref, species_ref, layer_hbm, bias_ref, out_ref,
           app_ref, whole_ref,
           gp, wave, pacc, part, prcv, cbf, layer, wpad, whi, wlo, mask, fold, bias_pad, lout_pad,
           dsend, drcv, dwide, dts, dflat, gs, scs, scr, appo, tmp,
           load_sem, keep_sem, xs, xr, ss, sr, zs, zr, cs, cr, ds_, dr, gs_s, gs_r):
    nb, ga, apd, K, nspec, hid = dims
    npair = nb // 2
    unit = 2 * apd
    qa = unit // ga
    q = qa * K
    qp = part.shape[2]
    rows = npair * qp
    blk = gp.shape[2]
    bands, gloc = wave.shape
    owned = npair * qa
    shift = qp.bit_length() - 1
    plane = npair == 4
    b = lax.axis_index("band")
    z = lax.axis_index("ga")
    chip, core = b // 2, b % 2

    def peer_chip(d):
        if plane:
            x, y = chip % 2, chip // 2
            x = 1 - x if d % 2 else x
            y = 1 - y if d // 2 else y
            return y * 2 + x
        return lax.rem(chip + d, npair)

    def from_chip(d):
        if plane:
            return peer_chip(d)
        return lax.rem(chip + npair - d, npair)

    sibling = chip * 2 + 1 - core
    width = gloc // PIECES

    def cols(i):
        return pl.ds(i * width, width)

    loads = [
        pltpu.make_async_copy(proj_hbm, gp.at[chip, core], load_sem.at[0]),
        pltpu.make_async_copy(wave_hbm, wave, load_sem.at[1]),
        pltpu.make_async_copy(layer_hbm, layer, load_sem.at[2]),
    ]
    for c in loads:
        c.start()

    barrier = pltpu.get_barrier_semaphore()
    for d in range(1, nb):
        pl.semaphore_signal(barrier, inc=1, device_id=(lax.rem(b + d, nb), z), device_id_type=MESH)
    for d in range(1, ga):
        pl.semaphore_signal(barrier, inc=1, device_id=(b, lax.rem(z + d, ga)), device_id_type=MESH)
    pl.semaphore_wait(barrier, nb + ga - 2)

    sends = []

    def remote(src, dst, send_sem, recv_sem, where):
        copy = pltpu.make_async_remote_copy(src_ref=src, dst_ref=dst, send_sem=send_sem, recv_sem=recv_sem,
                                            device_id=where, device_id_type=MESH)
        return copy

    def chip_copy(d, i, block_chip, target_chip, send_d):
        view = gp.at[block_chip, core, :, cols(i)]
        return remote(view, view, xs.at[send_d, i], xr.at[d, i], (target_chip * 2 + core, z))

    def sib_copy(d, i, block_chip):
        view = gp.at[block_chip, core, :, cols(i)]
        return remote(view, view, ss.at[d, i], sr.at[d, i], (sibling, z))

    def go(copy):
        copy.start()
        sends.append(copy)

    half = PIECES // 2
    order1 = list(range(PIECES))
    order2 = order1[half:] + order1[:half]
    loads[0].wait()
    for n in range(PIECES):
        if plane:
            go(chip_copy(1, order1[n], chip, peer_chip(1), 1))
            go(chip_copy(2, order2[n], chip, peer_chip(2), 2))
        else:
            for d in range(1, npair):
                go(chip_copy(d, n, chip, peer_chip(d), d))
    for n in range(PIECES):
        go(sib_copy(0, n, chip))

    wpad[...] = jnp.zeros_like(wpad)
    bias_pad[...] = jnp.zeros_like(bias_pad)
    lout_pad[...] = jnp.zeros_like(lout_pad)
    dwide[...] = jnp.zeros_like(dwide)
    gs[...] = jnp.zeros_like(gs)
    dflat[...] = jnp.zeros_like(dflat)
    tmp[...] = jnp.zeros_like(tmp)

    def place(i, axis_shape, axis):
        idx = lax.broadcasted_iota(jnp.int32, axis_shape, axis)
        pair = idx >> shift
        w = idx - (pair << shift)
        j = jnp.zeros_like(w)
        for t in range(1, qa):
            j = j + (w >= t * K).astype(jnp.int32)
        return pair * qa + j, w - j * K, w < q

    ar, _, vr = place(0, (rows, rows), 0)
    ac, _, vc = place(0, (rows, rows), 1)
    mask[...] = jnp.where((ar == ac) & vr & vc, 1.0, 0.0).astype(F32)
    _, kc, vk = place(0, (LPAD, rows), 1)
    lrow = lax.broadcasted_iota(jnp.int32, (LPAD, rows), 0)
    fold[...] = jnp.where((lrow == kc) & vk, 1.0, 0.0).astype(F32).astype(BF16)

    for s in range(nspec):
        bias_pad[0:1, s * 128:s * 128 + hid] = bias_ref[s:s + 1, :]
        lout_pad[0:1, s * 128:s * 128 + hid] = out_ref[s:s + 1, :]
    loads[2].wait()
    for s in range(nspec):
        for k in range(K):
            wpad[k * LPAD:k * LPAD + K, s * 128:s * 128 + hid] = layer[s, k * K:(k + 1) * K, :]
    high, low = split(wpad[...])
    whi[...] = high
    wlo[...] = low
    loads[1].wait()

    keeps = []
    ntile = 256 if bands % 256 == 0 else bands

    def project(stage, p):
        for c in range(2):
            k = pltpu.make_async_copy(gp.at[p, c], whole_ref.at[pl.ds(pl.multiple_of((p * 2 + c) * blk, blk), blk)],
                                      keep_sem.at[stage, c])
            k.start()
            keeps.append(k)
        lhs = gp[p].reshape(2 * blk, gloc)
        for t in range(bands // ntile):
            pacc[0:2 * blk, t * ntile:(t + 1) * ntile] = dot(lhs, wave[t * ntile:(t + 1) * ntile, :], (1, 1))
        live = lax.broadcasted_iota(jnp.int32, (qp, bands), 0) < q
        for r in range(ga):
            off = (r * qa) // apd * blk + (r * qa) % apd * K
            part[stage, r] = jnp.where(live, pacc[off:off + qp, :], 0.0).astype(BF16)
        for d in range(1, ga):
            to = lax.rem(z + d, ga)
            go(remote(part.at[stage, to], prcv.at[stage, d], zs.at[stage, d], zr.at[stage, d], (b, to)))

    def collect(stage, p):
        total = part[stage, z].astype(F32)
        for d in range(1, ga):
            pltpu.make_async_copy(prcv.at[stage, d], prcv.at[stage, d], zr.at[stage, d]).wait()
            total = total + prcv[stage, d].astype(F32)
        where = pl.ds(pl.multiple_of(p * qp, qp), qp)
        cbf[0, where, :] = total.astype(BF16)
        for d in range(1, ga):
            go(remote(cbf.at[0, where], cbf.at[d, where], cs.at[stage, d], cr.at[stage, d],
                      (b, lax.rem(z + d, ga))))

    def got_chip(d, i):
        view = gp.at[from_chip(d), core, :, cols(i)]
        pltpu.make_async_copy(view, view, xr.at[d, i]).wait()

    def got_sib(d, i):
        view = gp.at[from_chip(d), 1 - core, :, cols(i)]
        pltpu.make_async_copy(view, view, sr.at[d, i]).wait()

    def all_sib(d):
        for i in range(PIECES):
            got_sib(d, i)

    all_sib(0)
    project(0, chip)
    if plane:
        for n in range(PIECES):
            i, j = order1[n], order2[n]
            got_chip(1, i)
            if n < half:
                go(chip_copy(3, i, from_chip(1), peer_chip(2), 3))
            go(sib_copy(1, i, from_chip(1)))
            got_chip(2, j)
            if n < half:
                go(chip_copy(3, j, from_chip(2), peer_chip(1), 3))
            go(sib_copy(2, j, from_chip(2)))
        collect(0, chip)
        all_sib(1)
        project(1, from_chip(1))
        all_sib(2)
        project(2, from_chip(2))
        for n in range(half):
            for i in (order1[n], order2[n]):
                got_chip(3, i)
                go(sib_copy(3, i, from_chip(3)))
            if n == 0:
                collect(1, from_chip(1))
        collect(2, from_chip(2))
        all_sib(3)
        project(3, from_chip(3))
        collect(3, from_chip(3))
    else:
        for d in range(1, npair):
            for i in range(PIECES):
                got_chip(d, i)
                go(sib_copy(d, i, from_chip(d)))
            all_sib(d)
            project(d, from_chip(d))
            collect(d - 1, from_chip(d - 1))
        collect(npair - 1, from_chip(npair - 1))

    chi = cbf[0]
    wh, wl = split(chi.astype(F32) * occ_ref[...])
    gram = (dot(chi, wh, (1, 1)) + dot(chi, wl, (1, 1))) * mask[...]
    gh, gl = split(gram)
    dsend[...] = dot(fold[...], gh, (1, 0)) + dot(fold[...], gl, (1, 0))
    for d in range(1, nb):
        go(remote(dsend, drcv.at[d], ds_.at[d], dr.at[d], (lax.rem(b + d, nb), z)))

    arow = lax.broadcasted_iota(jnp.int32, (owned, nspec * 128), 0)
    lane_kind = lax.broadcasted_iota(jnp.int32, (owned, nspec * 128), 1) >> 7
    kind = jnp.zeros((owned, nspec * 128), jnp.int32)
    for j in range(qa):
        for p in range(npair):
            kind = jnp.where(arow == j * npair + p, species_ref[p * unit + z * qa + j], kind)
    onehot = jnp.where(kind == lane_kind, 1.0, 0.0).astype(F32)

    def pick(values):
        values = values * onehot
        return sum(values[:, s * 128:(s + 1) * 128] for s in range(nspec))

    bias_atom = pick(jnp.broadcast_to(bias_pad[0:1, :], onehot.shape))
    out_atom = pick(jnp.broadcast_to(lout_pad[0:1, :], onehot.shape))

    density = dsend[...]
    for d in range(1, nb):
        pltpu.make_async_copy(drcv.at[d], drcv.at[d], dr.at[d]).wait()
        density = density + drcv[d]
    dwide[0:LPAD, :] = density * (1.0 / (bands * nb))
    dts[...] = dwide[...].T
    for k in range(K):
        for j in range(qa):
            dflat[j * npair:(j + 1) * npair, k * LPAD:(k + 1) * LPAD] = \
                dts[pl.ds(j * K + k, npair, stride=qp), :][:, 0:LPAD]
    dh, dl = split(dflat[...])
    pre = pick(dot(dh, whi[...], (1, 0)) + dot(dl, whi[...], (1, 0)) + dot(dh, wlo[...], (1, 0))) + bias_atom
    act = jnp.tanh(pre)
    slopes = out_atom * (1.0 - act * act)
    sh, sl = split(jnp.concatenate([slopes] * nspec, axis=1) * onehot)
    grad = dot(sh, whi[...], (1, 1)) + dot(sl, whi[...], (1, 1)) + dot(sh, wlo[...], (1, 1))
    grad = jnp.concatenate([grad, jnp.zeros((owned, 128), F32)], axis=1)
    for k in range(K):
        for j in range(qa):
            gs[pl.ds(j * K + k, npair, stride=qp), :] = \
                grad[j * npair:(j + 1) * npair, k * LPAD:k * LPAD + 128]
    gh, gl = split(gs[:, 0:LPAD])
    wide = (dot(gh, fold[...], (1, 0)) + dot(gl, fold[...], (1, 0))) * mask[...]
    sym = wide + wide.T
    sh, sl = split(sym)
    scs[...] = dot(fold[...], sh, (1, 0)) + dot(fold[...], sl, (1, 0))
    for d in range(1, ga):
        go(remote(scs, scr.at[d], gs_s.at[d], gs_r.at[d], (b, lax.rem(z + d, ga))))

    factor = 1.0 / jnp.sqrt(F32(nb * apd * K))

    def apply(d, symm):
        sh, sl = split(symm)
        coefs = cbf[d]
        appo[lax.rem(z + ga - d, ga)] = (dot(sh, coefs, (1, 0)) + dot(sl, coefs, (1, 0))) * factor

    apply(0, sym)
    for d in range(1, ga):
        for stage in range(npair):
            where = pl.ds(pl.multiple_of(from_chip(stage) * qp, qp), qp)
            pltpu.make_async_copy(cbf.at[d, where], cbf.at[d, where], cr.at[stage, d]).wait()
        pltpu.make_async_copy(scr.at[d], scr.at[d], gs_r.at[d]).wait()
        sh, sl = split(scr[d])
        apply(d, (dot(fold[...], sh, (0, 0)) + dot(fold[...], sl, (0, 0))) * mask[...])

    for p in range(npair):
        for c in range(2):
            for r in range(c * apd // qa, (c + 1) * apd // qa):
                off = (r * qa) % apd * K
                tmp[off:off + q, :] = appo[r, p * qp:p * qp + q, :]
            app_ref[(p * 2 + c) * blk:(p * 2 + c + 1) * blk, :] = tmp[...].astype(BF16)

    for c in sends:
        c.wait_send()
    for k in keeps:
        k.wait()


def body(wave_coef, projector, occupation, species, layer_in, bias_in, layer_out):
    apd, K, gloc = projector.shape
    nb, ga = lax.axis_size("band"), lax.axis_size("ga")
    bands = wave_coef.shape[0]
    nspec, _, hid = layer_in.shape
    npair = nb // 2
    qa = 2 * apd // ga
    q = qa * K
    qp = 16
    while qp < q:
        qp *= 2
    blk = -(-apd * K // 16) * 16
    rows = npair * qp
    owned = npair * qa
    flat = -(-K * LPAD // 128) * 128
    own = jnp.pad(projector.reshape(apd * K, gloc), ((0, blk - apd * K), (0, 0)))
    vm = pl.BlockSpec(memory_space=pltpu.VMEM)
    hb = pl.BlockSpec(memory_space=pl.ANY)
    sem = pltpu.SemaphoreType.DMA
    app, whole = pl.pallas_call(
        functools.partial(kernel, (nb, ga, apd, K, nspec, hid)),
        out_shape=(
            jax.ShapeDtypeStruct((nb * blk, bands), BF16),
            jax.ShapeDtypeStruct((nb * blk, gloc), BF16),
        ),
        in_specs=[hb, hb, vm, pl.BlockSpec(memory_space=pltpu.SMEM), hb, vm, vm],
        out_specs=(vm, hb),
        scratch_shapes=[
            pltpu.VMEM((npair, 2, blk, gloc), BF16),
            pltpu.VMEM((bands, gloc), BF16),
            pltpu.VMEM((2 * blk + qp, bands), F32),
            pltpu.VMEM((npair, ga, qp, bands), BF16),
            pltpu.VMEM((npair, ga, qp, bands), BF16),
            pltpu.VMEM((ga, rows, bands), BF16),
            pltpu.VMEM(layer_in.shape, F32),
            pltpu.VMEM((flat, nspec * 128), F32),
            pltpu.VMEM((flat, nspec * 128), BF16),
            pltpu.VMEM((flat, nspec * 128), BF16),
            pltpu.VMEM((rows, rows), F32),
            pltpu.VMEM((LPAD, rows), BF16),
            pltpu.VMEM((8, nspec * 128), F32),
            pltpu.VMEM((8, nspec * 128), F32),
            pltpu.VMEM((LPAD, rows), F32),
            pltpu.VMEM((nb, LPAD, rows), F32),
            pltpu.VMEM((128, rows), F32),
            pltpu.VMEM((rows, 128), F32),
            pltpu.VMEM((owned, flat), F32),
            pltpu.VMEM((rows, 128), F32),
            pltpu.VMEM((LPAD, rows), F32),
            pltpu.VMEM((ga, LPAD, rows), F32),
            pltpu.VMEM((ga, rows, bands), F32),
            pltpu.VMEM((blk, bands), F32),
            sem((3,)),
            sem((npair, 2)),
            sem((npair, PIECES)), sem((npair, PIECES)),
            sem((npair, PIECES)), sem((npair, PIECES)),
            sem((npair, ga)), sem((npair, ga)),
            sem((npair, ga)), sem((npair, ga)),
            sem((nb,)), sem((nb,)),
            sem((ga,)), sem((ga,)),
        ],
        compiler_params=pltpu.CompilerParams(collective_id=0, has_side_effects=True,
                                             vmem_limit_bytes=56 * 1024 * 1024),
    )(wave_coef, own, occupation.reshape(1, bands), species, layer_in, bias_in, layer_out)
    corrected = lax.dot_general(app, whole, (((0,), (0,)), ((), ())), preferred_element_type=F32)
    return corrected.astype(BF16)


def solution(mesh):
    in_specs = (P("band", "ga"), P("band", None, "ga"), P("band"), P(), P(), P(), P())
    out_specs = P("band", "ga")
    return jax.shard_map(body, mesh=mesh, in_specs=in_specs, out_specs=out_specs, check_vma=False)
```

time: 195 us -> 95.1 us (0.49)
  waiting for transfers between devices: 92.5 us -> 0 us
  Pallas kernels: 0 us -> 79.5 us
  blocking collectives: 43.6 us -> 0 us
  matrix products: 41 us -> 9.97 us
  between operations: 13.5 us -> 0.03 us
  local copies, waits for them, and re-layouts: 3.39 us -> 5.46 us
    pallas_call x0 -> x1, Pallas kernels: none -> 79.5 us  [body(): pl.pallas_call(functools.partial(kernel, (nb, ga, apd, K, nspec, hid)), o...]
    all_gather x1 -> x0, waiting for transfers between devices: 57.1 us -> none  [body(): whole_proj = lax.all_gather(projector, 'band', axis=0, tiled=True)]
    reduce_scatter x1 -> x0, waiting for transfers between devices: 35.4 us -> none  [body(): lax.psum_scatter(partial_value, 'ga', scatter_dimension=1, tiled=True)]
    dot_general x9 -> x1, matrix products: 41 us -> 9.97 us  [body(): lax.dot_general(app, whole, (((0,), (0,)), ((), ())), preferred_element_t...]
    psum x1 -> x0, blocking collectives: 25 us -> none  [body(): density = lax.psum(local_density, 'band') / bands_all]
    all_gather x1 -> x0, blocking collectives: 18.6 us -> none  [body(): applied_all = lax.all_gather(applied, 'ga', axis=1, tiled=True)]
    unnamed x13 -> x2, local copies, waits for them, and re-layouts: 2.76 us -> 4.18 us
  transfers between devices with their start and end apart: 2 -> 0, of which waited for: 2 -> 0; matrix products, arithmetic and copies ran while one was open for 2% -> 0% of each run, Pallas kernels for 0% -> 0%
where the time goes in v1:
time: 95.1 us; the launch traced here: 94.9 us
  Pallas kernels  79.5 us (84%)
  matrix products  9.97 us (10%)
  local copies, waits for them, and re-layouts  5.46 us (6%)
    pallas_call x1, Pallas kernels, body(): pl.pallas_call(functools.partial(kernel, (nb, ga, apd, K, nspec, hid)), o...  79.5 us
    dot_general x1, matrix products, body(): lax.dot_general(app, whole, (((0,), (0,)), ((), ())), preferred_element_t...  9.97 us
    unnamed x2, local copies, waits for them, and re-layouts  4.18 us

profile of v1, /device:TPU:0, one launch (start us, length us, event | category | flops | bytes accessed | tf_op | source)
XLA Modules:
  0.0 94.9 jit_solution(8298582367941566191)
XLA Ops:
  0.0 1.7 %copy.10 = bf16[4,27,4096]{2,1,0:T(8,128)(2,1)S(1)} copy(bf16[4,27,4096]{2,0,1:T(4,128)(2,1)} %param.8) | data formatting | bytes 1769472 | tf_op args[1]
  1.7 0.3 reshape.6
  1.9 1.0 %pad.4.proj_hbm = bf16[112,4096]{1,0:T(8,128)(2,1)} pad(bf16[108,4096]{1,0:T(8,128)(2,1)S(1)} %reshape.6, bf16[]{:T(256)} %constant.2.clone.1), padding=0_4x0_0 | pad | bytes 1802242 | tf_op jit(solution)/shard_map/jit(_pad)/pad | solution.py:327
  3.0 2.5 %copy.11.layer_hbm = f32[4,729,100]{2,1,0:T(8,128)} copy(f32[4,729,100]{1,0,2:T(4,128)} %param.11) | data formatting | bytes 2332800 | tf_op args[4]
  5.5 79.5 %shard_map.73 = (bf16[896,512]{1,0:T(8,128)(2,1)}, bf16[896,4096]{1,0:T(8,128)(2,1)}) custom-call(bf16[512,4096]{1,0:T(8,128)(2,1)} %wave_hbm.1, bf16[112,4096]{1,0:T(8,128)(2,1)} %pad.4.proj_hbm, f32[1,512]{1,0:T(1,128)} %bitcast.3, s32[32]{0:T(128)} %species_ref.1, f32[4,729,100]{2,1,0:T(8,128)} %copy.11.layer_hbm, f32[4,100]{1,0:T(4,128)} %bias_ref.1, ...), custom_call_target="tpu_custom_call" | custom-call | tf_op jit(solution)/shard_map/pallas_call | solution.py:331
  84.9 10.0 %convolution_convert_fusion = bf16[512,4096]{1,0:T(8,128)(2,1)} fusion(bf16[896,512]{1,0:T(8,128)(2,1)} %get-tuple-element.7, bf16[896,4096]{1,0:T(8,128)(2,1)} %get-tuple-element.8), kind=kOutput, calls=%fused_computation | convolution fusion | flops 3760193536 | bytes 12451840 | tf_op jit(solution)/shard_map/dot_general | solution.py:376

commit v2 on v1

--- a/solution.py
+++ b/solution.py
@@ -27,7 +27,7 @@
            app_ref, whole_ref,
            gp, wave, pacc, part, prcv, cbf, layer, wpad, whi, wlo, mask, fold, bias_pad, lout_pad,
            dsend, drcv, dwide, dts, dflat, gs, scs, scr, appo, tmp,
-           load_sem, keep_sem, xs, xr, ss, sr, zs, zr, cs, cr, ds_, dr, gs_s, gs_r):
+           slot, mine, wide_in, turned, load_sem, keep_sem, xs, xr, ss, sr, zs, zr, cs, cr, ds_, dr, gs_s, gs_r):
     nb, ga, apd, K, nspec, hid = dims
     npair = nb // 2
     unit = 2 * apd
@@ -118,6 +118,8 @@
     gs[...] = jnp.zeros_like(gs)
     dflat[...] = jnp.zeros_like(dflat)
     tmp[...] = jnp.zeros_like(tmp)
+    slot[...] = jnp.zeros_like(slot)
+    wide_in[...] = jnp.zeros_like(wide_in)
 
     def place(i, axis_shape, axis):
         idx = lax.broadcasted_iota(jnp.int32, axis_shape, axis)
@@ -140,8 +142,10 @@
         lout_pad[0:1, s * 128:s * 128 + hid] = out_ref[s:s + 1, :]
     loads[2].wait()
     for s in range(nspec):
+        wide_in[0:hid, 0:K * K] = layer[:, s, :]
+        turned[...] = wide_in[...].T
         for k in range(K):
-            wpad[k * LPAD:k * LPAD + K, s * 128:s * 128 + hid] = layer[s, k * K:(k + 1) * K, :]
+            wpad[k * LPAD:k * LPAD + K, s * 128:(s + 1) * 128] = turned[k * K:(k + 1) * K, :]
     high, low = split(wpad[...])
     whi[...] = high
     wlo[...] = low
@@ -158,25 +162,95 @@
             keeps.append(k)
         lhs = gp[p].reshape(2 * blk, gloc)
         for t in range(bands // ntile):
-            pacc[0:2 * blk, t * ntile:(t + 1) * ntile] = dot(lhs, wave[t * ntile:(t + 1) * ntile, :], (1, 1))
-        live = lax.broadcasted_iota(jnp.int32, (qp, bands), 0) < q
+            piece = dot(lhs, wave[t * ntile:(t + 1) * ntile, :], (1, 1))
+            for u in range(ntile // 128):
+                pacc[t * (ntile // 128) + u] = piece[:, u * 128:(u + 1) * 128]
+        own = None
         for r in range(ga):
-            off = (r * qa) // apd * blk + (r * qa) % apd * K
-            part[stage, r] = jnp.where(live, pacc[off:off + qp, :], 0.0).astype(BF16)
-        for d in range(1, ga):
-            to = lax.rem(z + d, ga)
-            go(remote(part.at[stage, to], prcv.at[stage, d], zs.at[stage, d], zr.at[stage, d], (b, to)))
+            for j in range(qa):
+                atom = (r * qa + j) % apd
+                base = (r * qa + j) // apd * blk + atom
+                for u in range(bands // 128):
+                    slot[j * K:(j + 1) * K, u * 128:(u + 1) * 128] = pacc[u, pl.ds(base, K, stride=apd), :]
+            value = slot[...]
+            part[stage, r] = value.astype(BF16)
+            own = value if own is None else jnp.where(z == r, value, own)
+        mine[stage] = own
+        at_end(0, lambda: [push(0, stage, r, 0) for r in range(1, ga)])
+        at_end(ga - 1, lambda: [push(1, stage, r, ga - 1) for r in range(ga - 1)])
+
+    line_sends = [[] for _ in range(ga)]
+
+    def at_end(v, work):
+        @pl.when(z == v)
+        def _():
+            work()
+
+    def push(way, stage, r, v):
+        to = v + 1 if way == 0 else v - 1
+
+        def make():
+            return remote(part.at[stage, r], prcv.at[way, stage, r], zs.at[stage, r], zr.at[way, stage, r], (b, to))
+        make().start()
+        line_sends[v].append(make)
+
+    def arrive(way, stage, r):
+        view = prcv.at[way, stage, r]
+        pltpu.make_async_copy(view, view, zr.at[way, stage, r]).wait()
+        return prcv[way, stage, r].astype(F32)
+
+    def both_ways(v):
+        return (0, 1) if v < ga // 2 else (1, 0)
+
+    def hop(stage):
+        def work(v):
+            for way in both_ways(v):
+                for r in (range(v + 1, ga) if way == 0 else range(v)):
+                    part[stage, r] = (part[stage, r].astype(F32) + arrive(way, stage, r)).astype(BF16)
+                    push(way, stage, r, v)
+        for v in range(1, ga - 1):
+            at_end(v, functools.partial(work, v))
+
+    def share(way, p, stage, r, v):
+        to = v + 1 if way == 0 else v - 1
+
+        def make():
+            view = cbf.at[r, place_of(p)]
+            return remote(view, view, cs.at[way, stage, r], cr.at[stage, r], (b, to))
+        make().start()
+        line_sends[v].append(make)
+
+    def place_of(p):
+        return pl.ds(pl.multiple_of(p * qp, qp), qp)
 
     def collect(stage, p):
-        total = part[stage, z].astype(F32)
-        for d in range(1, ga):
-            pltpu.make_async_copy(prcv.at[stage, d], prcv.at[stage, d], zr.at[stage, d]).wait()
-            total = total + prcv[stage, d].astype(F32)
-        where = pl.ds(pl.multiple_of(p * qp, qp), qp)
-        cbf[0, where, :] = total.astype(BF16)
-        for d in range(1, ga):
-            go(remote(cbf.at[0, where], cbf.at[d, where], cs.at[stage, d], cr.at[stage, d],
-                      (b, lax.rem(z + d, ga))))
+        def work(v):
+            total = mine[stage]
+            if v > 0:
+                total = total + arrive(0, stage, v)
+            if v < ga - 1:
+                total = total + arrive(1, stage, v)
+            cbf[v, place_of(p), :] = total.astype(BF16)
+            if v > 0:
+                share(1, p, stage, v, v)
+            if v < ga - 1:
+                share(0, p, stage, v, v)
+        for v in range(ga):
+            at_end(v, functools.partial(work, v))
+
+    def got_share(stage, p, r):
+        view = cbf.at[r, place_of(p)]
+        pltpu.make_async_copy(view, view, cr.at[stage, r]).wait()
+
+    def spread(stage, p):
+        def work(v):
+            for way in both_ways(v):
+                for r in (range(v - 1, -1, -1) if way == 0 else range(v + 1, ga)):
+                    got_share(stage, p, r)
+                    if 0 < v < ga - 1:
+                        share(way, p, stage, r, v)
+        for v in range(ga):
+            at_end(v, functools.partial(work, v))
 
     def got_chip(d, i):
         view = gp.at[from_chip(d), core, :, cols(i)]
@@ -203,20 +277,29 @@
             if n < half:
                 go(chip_copy(3, j, from_chip(2), peer_chip(1), 3))
             go(sib_copy(2, j, from_chip(2)))
-        collect(0, chip)
+            if n == 1:
+                hop(0)
+            if n == 2:
+                collect(0, chip)
         all_sib(1)
         project(1, from_chip(1))
         all_sib(2)
         project(2, from_chip(2))
+        spread(0, chip)
+        hop(1)
         for n in range(half):
             for i in (order1[n], order2[n]):
                 got_chip(3, i)
                 go(sib_copy(3, i, from_chip(3)))
             if n == 0:
+                hop(2)
                 collect(1, from_chip(1))
         collect(2, from_chip(2))
         all_sib(3)
         project(3, from_chip(3))
+        spread(1, from_chip(1))
+        spread(2, from_chip(2))
+        hop(3)
         collect(3, from_chip(3))
     else:
         for d in range(1, npair):
@@ -225,10 +308,13 @@
                 go(sib_copy(d, i, from_chip(d)))
             all_sib(d)
             project(d, from_chip(d))
+            hop(d - 1)
             collect(d - 1, from_chip(d - 1))
+            spread(d - 1, from_chip(d - 1))
+        hop(npair - 1)
         collect(npair - 1, from_chip(npair - 1))
 
-    chi = cbf[0]
+    chi = cbf[z]
     wh, wl = split(chi.astype(F32) * occ_ref[...])
     gram = (dot(chi, wh, (1, 1)) + dot(chi, wl, (1, 1))) * mask[...]
     gh, gl = split(gram)
@@ -251,6 +337,7 @@
     bias_atom = pick(jnp.broadcast_to(bias_pad[0:1, :], onehot.shape))
     out_atom = pick(jnp.broadcast_to(lout_pad[0:1, :], onehot.shape))
 
+    spread(npair - 1, from_chip(npair - 1))
     density = dsend[...]
     for d in range(1, nb):
         pltpu.make_async_copy(drcv.at[d], drcv.at[d], dr.at[d]).wait()
@@ -284,27 +371,30 @@
 
     def apply(d, symm):
         sh, sl = split(symm)
-        coefs = cbf[d]
-        appo[lax.rem(z + ga - d, ga)] = (dot(sh, coefs, (1, 0)) + dot(sl, coefs, (1, 0))) * factor
+        owner = lax.rem(z + ga - d, ga)
+        coefs = cbf[owner]
+        appo[owner] = (dot(sh, coefs, (1, 0)) + dot(sl, coefs, (1, 0))) * factor
 
     apply(0, sym)
     for d in range(1, ga):
-        for stage in range(npair):
-            where = pl.ds(pl.multiple_of(from_chip(stage) * qp, qp), qp)
-            pltpu.make_async_copy(cbf.at[d, where], cbf.at[d, where], cr.at[stage, d]).wait()
         pltpu.make_async_copy(scr.at[d], scr.at[d], gs_r.at[d]).wait()
         sh, sl = split(scr[d])
         apply(d, (dot(fold[...], sh, (0, 0)) + dot(fold[...], sl, (0, 0))) * mask[...])
 
     for p in range(npair):
         for c in range(2):
-            for r in range(c * apd // qa, (c + 1) * apd // qa):
-                off = (r * qa) % apd * K
-                tmp[off:off + q, :] = appo[r, p * qp:p * qp + q, :]
-            app_ref[(p * 2 + c) * blk:(p * 2 + c + 1) * blk, :] = tmp[...].astype(BF16)
+            for a in range(apd):
+                r, j = (c * apd + a) // qa, (c * apd + a) % qa
+                for u in range(bands // 128):
+                    tmp[u, pl.ds(a, K, stride=apd), :] = \
+                        appo[r, p * qp + j * K:p * qp + (j + 1) * K, u * 128:(u + 1) * 128]
+            for u in range(bands // 128):
+                app_ref[(p * 2 + c) * blk:(p * 2 + c + 1) * blk, u * 128:(u + 1) * 128] = tmp[u].astype(BF16)
 
     for c in sends:
         c.wait_send()
+    for v in range(ga):
+        at_end(v, lambda: [make().wait_send() for make in line_sends[v]])
     for k in keeps:
         k.wait()
 
@@ -324,7 +414,7 @@
     rows = npair * qp
     owned = npair * qa
     flat = -(-K * LPAD // 128) * 128
-    own = jnp.pad(projector.reshape(apd * K, gloc), ((0, blk - apd * K), (0, 0)))
+    own = jnp.pad(jnp.swapaxes(projector, 0, 1).reshape(apd * K, gloc), ((0, blk - apd * K), (0, 0)))
     vm = pl.BlockSpec(memory_space=pltpu.VMEM)
     hb = pl.BlockSpec(memory_space=pl.ANY)
     sem = pltpu.SemaphoreType.DMA
@@ -339,11 +429,11 @@
         scratch_shapes=[
             pltpu.VMEM((npair, 2, blk, gloc), BF16),
             pltpu.VMEM((bands, gloc), BF16),
-            pltpu.VMEM((2 * blk + qp, bands), F32),
+            pltpu.VMEM((bands // 128, 2 * blk, 128), F32),
             pltpu.VMEM((npair, ga, qp, bands), BF16),
-            pltpu.VMEM((npair, ga, qp, bands), BF16),
+            pltpu.VMEM((2, npair, ga, qp, bands), BF16),
             pltpu.VMEM((ga, rows, bands), BF16),
-            pltpu.VMEM(layer_in.shape, F32),
+            pltpu.VMEM((hid, nspec, K * K), F32),
             pltpu.VMEM((flat, nspec * 128), F32),
             pltpu.VMEM((flat, nspec * 128), BF16),
             pltpu.VMEM((flat, nspec * 128), BF16),
@@ -360,19 +450,23 @@
             pltpu.VMEM((LPAD, rows), F32),
             pltpu.VMEM((ga, LPAD, rows), F32),
             pltpu.VMEM((ga, rows, bands), F32),
-            pltpu.VMEM((blk, bands), F32),
+            pltpu.VMEM((bands // 128, blk, 128), F32),
+            pltpu.VMEM((qp, bands), F32),
+            pltpu.VMEM((npair, qp, bands), F32),
+            pltpu.VMEM((128, -(-K * K // 128) * 128), F32),
+            pltpu.VMEM((-(-K * K // 128) * 128, 128), F32),
             sem((3,)),
             sem((npair, 2)),
             sem((npair, PIECES)), sem((npair, PIECES)),
             sem((npair, PIECES)), sem((npair, PIECES)),
-            sem((npair, ga)), sem((npair, ga)),
-            sem((npair, ga)), sem((npair, ga)),
+            sem((npair, ga)), sem((2, npair, ga)),
+            sem((2, npair, ga)), sem((npair, ga)),
             sem((nb,)), sem((nb,)),
             sem((ga,)), sem((ga,)),
         ],
         compiler_params=pltpu.CompilerParams(collective_id=0, has_side_effects=True,
                                              vmem_limit_bytes=56 * 1024 * 1024),
-    )(wave_coef, own, occupation.reshape(1, bands), species, layer_in, bias_in, layer_out)
+    )(wave_coef, own, occupation.reshape(1, bands), species, jnp.transpose(layer_in, (2, 0, 1)), bias_in, layer_out)
     corrected = lax.dot_general(app, whole, (((0,), (0,)), ((), ())), preferred_element_type=F32)
     return corrected.astype(BF16)
 

time: 95.1 us -> 96.9 us (1.019)
  Pallas kernels: 79.5 us -> 84.1 us
  local copies, waits for them, and re-layouts: 5.46 us -> 2.64 us
    pallas_call x1, Pallas kernels: 79.5 us -> 84.1 us  [body(): pl.pallas_call(functools.partial(kernel, (nb, ga, apd, K, nspec, hid)), o...]
    unnamed x2 -> x0, local copies, waits for them, and re-layouts: 4.18 us -> none
    reshape x1, local copies, waits for them, and re-layouts: 0.27 us -> 1.63 us  [body(): jnp.swapaxes(projector, 0, 1).reshape(apd * K, gloc)]
where the time goes in v2:
time: 96.9 us; the launch traced here: 96.7 us
  Pallas kernels  84.1 us (87%)
  matrix products  9.97 us (10%)
  local copies, waits for them, and re-layouts  2.64 us (3%)
    pallas_call x1, Pallas kernels, body(): pl.pallas_call(functools.partial(kernel, (nb, ga, apd, K, nspec, hid)), o...  84.1 us
    dot_general x1, matrix products, body(): lax.dot_general(app, whole, (((0,), (0,)), ((), ())), preferred_element_t...  9.97 us

profile of v2, /device:TPU:0, one launch (start us, length us, event | category | flops | bytes accessed | tf_op | source)
XLA Modules:
  0.0 96.7 jit_solution(17104266875624563406)
XLA Ops:
  0.0 1.6 %reshape.6 = bf16[108,4096]{1,0:T(8,128)(2,1)S(1)} reshape(bf16[27,4,4096]{2,1,0:T(4,128)(2,1)} %bitcast.6) | data formatting | bytes 1769472 | tf_op jit(solution)/shard_map/reshape | solution.py:417
  1.6 1.0 %pad.4.proj_hbm = bf16[112,4096]{1,0:T(8,128)(2,1)} pad(bf16[108,4096]{1,0:T(8,128)(2,1)S(1)} %reshape.6, bf16[]{:T(256)} %constant.2.clone.1), padding=0_4x0_0 | pad | bytes 1802242 | tf_op jit(solution)/shard_map/jit(_pad)/pad | solution.py:417
  2.6 84.1 %shard_map.73 = (bf16[896,512]{1,0:T(8,128)(2,1)}, bf16[896,4096]{1,0:T(8,128)(2,1)}) custom-call(bf16[512,4096]{1,0:T(8,128)(2,1)} %wave_hbm.1, bf16[112,4096]{1,0:T(8,128)(2,1)} %pad.4.proj_hbm, f32[1,512]{1,0:T(1,128)} %bitcast.7, s32[32]{0:T(128)} %species_ref.1, f32[100,4,729]{2,1,0:T(4,128)} %bitcast.5, f32[4,100]{1,0:T(4,128)} %bias_ref.1, ...), custom_call_target="tpu_custom_call" | custom-call | tf_op jit(solution)/shard_map/pallas_call | solution.py:421
  86.8 10.0 %convolution_convert_fusion = bf16[512,4096]{1,0:T(8,128)(2,1)} fusion(bf16[896,512]{1,0:T(8,128)(2,1)} %get-tuple-element.7, bf16[896,4096]{1,0:T(8,128)(2,1)} %get-tuple-element.8), kind=kOutput, calls=%fused_computation | convolution fusion | flops 3760193536 | bytes 12451840 | tf_op jit(solution)/shard_map/dot_general | solution.py:470

commit v3 on v1

--- a/solution.py
+++ b/solution.py
@@ -27,7 +27,7 @@
            app_ref, whole_ref,
            gp, wave, pacc, part, prcv, cbf, layer, wpad, whi, wlo, mask, fold, bias_pad, lout_pad,
            dsend, drcv, dwide, dts, dflat, gs, scs, scr, appo, tmp,
-           load_sem, keep_sem, xs, xr, ss, sr, zs, zr, cs, cr, ds_, dr, gs_s, gs_r):
+           slot, wide_in, turned, load_sem, keep_sem, xs, xr, ss, sr, zs, zr, cs, cr, ds_, dr, gs_s, gs_r):
     nb, ga, apd, K, nspec, hid = dims
     npair = nb // 2
     unit = 2 * apd
@@ -118,6 +118,8 @@
     gs[...] = jnp.zeros_like(gs)
     dflat[...] = jnp.zeros_like(dflat)
     tmp[...] = jnp.zeros_like(tmp)
+    slot[...] = jnp.zeros_like(slot)
+    wide_in[...] = jnp.zeros_like(wide_in)
 
     def place(i, axis_shape, axis):
         idx = lax.broadcasted_iota(jnp.int32, axis_shape, axis)
@@ -140,8 +142,10 @@
         lout_pad[0:1, s * 128:s * 128 + hid] = out_ref[s:s + 1, :]
     loads[2].wait()
     for s in range(nspec):
+        wide_in[0:hid, 0:K * K] = layer[:, s, :]
+        turned[...] = wide_in[...].T
         for k in range(K):
-            wpad[k * LPAD:k * LPAD + K, s * 128:s * 128 + hid] = layer[s, k * K:(k + 1) * K, :]
+            wpad[k * LPAD:k * LPAD + K, s * 128:(s + 1) * 128] = turned[k * K:(k + 1) * K, :]
     high, low = split(wpad[...])
     whi[...] = high
     wlo[...] = low
@@ -158,11 +162,16 @@
             keeps.append(k)
         lhs = gp[p].reshape(2 * blk, gloc)
         for t in range(bands // ntile):
-            pacc[0:2 * blk, t * ntile:(t + 1) * ntile] = dot(lhs, wave[t * ntile:(t + 1) * ntile, :], (1, 1))
-        live = lax.broadcasted_iota(jnp.int32, (qp, bands), 0) < q
+            piece = dot(lhs, wave[t * ntile:(t + 1) * ntile, :], (1, 1))
+            for u in range(ntile // 128):
+                pacc[t * (ntile // 128) + u] = piece[:, u * 128:(u + 1) * 128]
         for r in range(ga):
-            off = (r * qa) // apd * blk + (r * qa) % apd * K
-            part[stage, r] = jnp.where(live, pacc[off:off + qp, :], 0.0).astype(BF16)
+            for j in range(qa):
+                atom = (r * qa + j) % apd
+                base = (r * qa + j) // apd * blk + atom
+                for u in range(bands // 128):
+                    slot[j * K:(j + 1) * K, u * 128:(u + 1) * 128] = pacc[u, pl.ds(base, K, stride=apd), :]
+            part[stage, r] = slot[...].astype(BF16)
         for d in range(1, ga):
             to = lax.rem(z + d, ga)
             go(remote(part.at[stage, to], prcv.at[stage, d], zs.at[stage, d], zr.at[stage, d], (b, to)))
@@ -212,11 +221,10 @@
             for i in (order1[n], order2[n]):
                 got_chip(3, i)
                 go(sib_copy(3, i, from_chip(3)))
-            if n == 0:
-                collect(1, from_chip(1))
-        collect(2, from_chip(2))
         all_sib(3)
         project(3, from_chip(3))
+        collect(1, from_chip(1))
+        collect(2, from_chip(2))
         collect(3, from_chip(3))
     else:
         for d in range(1, npair):
@@ -298,15 +306,26 @@
 
     for p in range(npair):
         for c in range(2):
-            for r in range(c * apd // qa, (c + 1) * apd // qa):
-                off = (r * qa) % apd * K
-                tmp[off:off + q, :] = appo[r, p * qp:p * qp + q, :]
-            app_ref[(p * 2 + c) * blk:(p * 2 + c + 1) * blk, :] = tmp[...].astype(BF16)
+            for a in range(apd):
+                r, j = (c * apd + a) // qa, (c * apd + a) % qa
+                for u in range(bands // 128):
+                    tmp[u, pl.ds(a, K, stride=apd), :] = \
+                        appo[r, p * qp + j * K:p * qp + (j + 1) * K, u * 128:(u + 1) * 128]
+            for u in range(bands // 128):
+                app_ref[(p * 2 + c) * blk:(p * 2 + c + 1) * blk, u * 128:(u + 1) * 128] = tmp[u].astype(BF16)
 
     for c in sends:
         c.wait_send()
     for k in keeps:
         k.wait()
+
+
+def expand(app_ref, whole_ref, out_ref, turned):
+    @pl.when(pl.program_id(0) == 0)
+    def _():
+        turned[...] = app_ref[...].T
+
+    out_ref[...] = dot(turned[...], whole_ref[...], (1, 0)).astype(BF16)
 
 
 def body(wave_coef, projector, occupation, species, layer_in, bias_in, layer_out):
@@ -324,7 +343,7 @@
     rows = npair * qp
     owned = npair * qa
     flat = -(-K * LPAD // 128) * 128
-    own = jnp.pad(projector.reshape(apd * K, gloc), ((0, blk - apd * K), (0, 0)))
+    own = jnp.pad(jnp.swapaxes(projector, 0, 1).reshape(apd * K, gloc), ((0, blk - apd * K), (0, 0)))
     vm = pl.BlockSpec(memory_space=pltpu.VMEM)
     hb = pl.BlockSpec(memory_space=pl.ANY)
     sem = pltpu.SemaphoreType.DMA
@@ -339,11 +358,11 @@
         scratch_shapes=[
             pltpu.VMEM((npair, 2, blk, gloc), BF16),
             pltpu.VMEM((bands, gloc), BF16),
-            pltpu.VMEM((2 * blk + qp, bands), F32),
+            pltpu.VMEM((bands // 128, 2 * blk, 128), F32),
             pltpu.VMEM((npair, ga, qp, bands), BF16),
             pltpu.VMEM((npair, ga, qp, bands), BF16),
             pltpu.VMEM((ga, rows, bands), BF16),
-            pltpu.VMEM(layer_in.shape, F32),
+            pltpu.VMEM((hid, nspec, K * K), F32),
             pltpu.VMEM((flat, nspec * 128), F32),
             pltpu.VMEM((flat, nspec * 128), BF16),
             pltpu.VMEM((flat, nspec * 128), BF16),
@@ -360,7 +379,10 @@
             pltpu.VMEM((LPAD, rows), F32),
             pltpu.VMEM((ga, LPAD, rows), F32),
             pltpu.VMEM((ga, rows, bands), F32),
-            pltpu.VMEM((blk, bands), F32),
+            pltpu.VMEM((bands // 128, blk, 128), F32),
+            pltpu.VMEM((qp, bands), F32),
+            pltpu.VMEM((128, -(-K * K // 128) * 128), F32),
+            pltpu.VMEM((-(-K * K // 128) * 128, 128), F32),
             sem((3,)),
             sem((npair, 2)),
             sem((npair, PIECES)), sem((npair, PIECES)),
@@ -372,9 +394,20 @@
         ],
         compiler_params=pltpu.CompilerParams(collective_id=0, has_side_effects=True,
                                              vmem_limit_bytes=56 * 1024 * 1024),
-    )(wave_coef, own, occupation.reshape(1, bands), species, layer_in, bias_in, layer_out)
-    corrected = lax.dot_general(app, whole, (((0,), (0,)), ((), ())), preferred_element_type=F32)
-    return corrected.astype(BF16)
+    )(wave_coef, own, occupation.reshape(1, bands), species, jnp.transpose(layer_in, (2, 0, 1)), bias_in, layer_out)
+    tile = 512 if gloc % 512 == 0 else gloc
+    return pl.pallas_call(
+        expand,
+        grid=(gloc // tile,),
+        out_shape=jax.ShapeDtypeStruct((bands, gloc), BF16),
+        in_specs=[
+            pl.BlockSpec((nb * blk, bands), lambda i: (0, 0)),
+            pl.BlockSpec((nb * blk, tile), lambda i: (0, i)),
+        ],
+        out_specs=pl.BlockSpec((bands, tile), lambda i: (0, i)),
+        scratch_shapes=[pltpu.VMEM((bands, nb * blk), BF16)],
+        compiler_params=pltpu.CompilerParams(vmem_limit_bytes=32 * 1024 * 1024),
+    )(app, whole)
 
 
 def solution(mesh):

time: 95.1 us -> 89.3 us (0.939)
  matrix products: 9.97 us -> 0 us
  Pallas kernels: 79.5 us -> 82.2 us
  local copies, waits for them, and re-layouts: 5.46 us -> 6.89 us
    dot_general x1 -> x0, matrix products: 9.97 us -> none  [body(): lax.dot_general(app, whole, (((0,), (0,)), ((), ())), preferred_element_t...]
    pallas_call x0 -> x1, Pallas kernels: none -> 7.41 us  [body(): pl.pallas_call(expand, grid=(gloc // tile,), out_shape=jax.ShapeDtypeStru...]
    pallas_call x1, Pallas kernels: 79.5 us -> 74.8 us  [body(): pl.pallas_call(functools.partial(kernel, (nb, ga, apd, K, nspec, hid)), o...]
    reshape x1, local copies, waits for them, and re-layouts: 0.27 us -> 1.63 us  [body(): jnp.swapaxes(projector, 0, 1).reshape(apd * K, gloc)]
    unnamed x2 -> x4, local copies, waits for them, and re-layouts: 4.18 us -> 4.25 us
where the time goes in v3:
time: 89.3 us; the launch traced here: 89.1 us
  Pallas kernels  82.2 us (92%)
  local copies, waits for them, and re-layouts  6.89 us (8%)
    pallas_call x1, Pallas kernels, body(): pl.pallas_call(functools.partial(kernel, (nb, ga, apd, K, nspec, hid)), o...  74.8 us
    pallas_call x1, Pallas kernels, body(): pl.pallas_call(expand, grid=(gloc // tile,), out_shape=jax.ShapeDtypeStru...  7.41 us
    unnamed x4, local copies, waits for them, and re-layouts  4.25 us

profile of v3, /device:TPU:0, one launch (start us, length us, event | category | flops | bytes accessed | tf_op | source)
XLA Modules:
  0.0 89.1 jit_solution(3402222878306935031)
XLA Ops:
  0.0 1.6 %reshape.6 = bf16[108,4096]{1,0:T(8,128)(2,1)S(1)} reshape(bf16[27,4,4096]{2,1,0:T(4,128)(2,1)} %bitcast.4) | data formatting | bytes 1769472 | tf_op jit(solution)/shard_map/reshape | solution.py:346
  1.6 1.0 %pad.4.proj_hbm = bf16[112,4096]{1,0:T(8,128)(2,1)} pad(bf16[108,4096]{1,0:T(8,128)(2,1)S(1)} %reshape.6, bf16[]{:T(256)} %constant.2.clone.1), padding=0_4x0_0 | pad | bytes 1802242 | tf_op jit(solution)/shard_map/jit(_pad)/pad | solution.py:346
  2.6 74.8 %shard_map.73 = (bf16[896,512]{1,0:T(8,128)(2,1)}, bf16[896,4096]{1,0:T(8,128)(2,1)}) custom-call(bf16[512,4096]{1,0:T(8,128)(2,1)} %wave_hbm.1, bf16[112,4096]{1,0:T(8,128)(2,1)} %pad.4.proj_hbm, f32[1,512]{1,0:T(1,128)} %bitcast.5, s32[32]{0:T(128)} %species_ref.1, f32[100,4,729]{2,1,0:T(4,128)} %bitcast.3, f32[4,100]{1,0:T(4,128)} %bias_ref.1, ...), custom_call_target="tpu_custom_call" | custom-call | tf_op jit(solution)/shard_map/pallas_call | solution.py:350
  77.4 0.0 copy-start
  77.4 3.1 %copy-done = bf16[896,4096]{1,0:T(8,128)(2,1)S(1)} copy-done((bf16[896,4096]{1,0:T(8,128)(2,1)S(1)}, bf16[896,4096]{1,0:T(8,128)(2,1)}, u32[]{:S(2)}) %copy-start) | copy-done | bytes 7340056
  80.5 0.0 copy-start.1
  80.5 1.2 %copy-done.1 = bf16[896,512]{1,0:T(8,128)(2,1)S(1)} copy-done((bf16[896,512]{1,0:T(8,128)(2,1)S(1)}, bf16[896,512]{1,0:T(8,128)(2,1)}, u32[]{:S(2)}) %copy-start.1) | copy-done | bytes 917528
  81.7 7.4 %shard_map.74 = bf16[512,4096]{1,0:T(8,128)(2,1)} custom-call(bf16[896,512]{1,0:T(8,128)(2,1)S(1)} %copy-done.1, bf16[896,4096]{1,0:T(8,128)(2,1)S(1)} %copy-done), custom_call_target="tpu_custom_call" | custom-call | tf_op jit(solution)/shard_map/pallas_call | solution.py:399
Async XLA Ops:
  77.4 3.1 %copy-start = (bf16[896,4096]{1,0:T(8,128)(2,1)S(1)}, bf16[896,4096]{1,0:T(8,128)(2,1)}, u32[]{:S(2)}) copy-start(bf16[896,4096]{1,0:T(8,128)(2,1)} %get-tuple-element.8.whole_ref) | copy-start | bytes 22020100
  80.5 1.2 %copy-start.1 = (bf16[896,512]{1,0:T(8,128)(2,1)S(1)}, bf16[896,512]{1,0:T(8,128)(2,1)}, u32[]{:S(2)}) copy-start(bf16[896,512]{1,0:T(8,128)(2,1)} %get-tuple-element.7.app_ref) | copy-start | bytes 2752516
